TPU v7x, 32 devices: a whole 2x2x4 slice. The times are simulated.
32 devices in a mesh: member: 4 (over y, core), space: 8 (over z, x).
Axes of the slice: x: 2, y: 2, z: 4, core: 2. Of those that a mesh axis runs over, the one named last changes fastest.
Arguments:
- participant_swirls: float32 [8, 512, 512], P('member', 'space'), may hold values from -6 to 6
- driving_source: float32 [512, 512], P('space'), may hold values from -12 to 12
- mixing: float32 [8, 8], replicated, may hold values from -2 to 2
- probes: int32 [16384], P('space'), may hold values from 0 to 32767
- observed: float32 [16384], P('space'), may hold values from -6 to 6
Outputs:
- analysis: float32 [8, 512, 512], P('member', 'space')
- spread: float32 [8, 8], replicated
- projection: float32 [8], replicated
Inputs may be any that keep to these rules, and one draw needn't show every extreme that they name: `probes`: each index names a cell of its own block's 64 rows, row-major with 512 columns.
All inputs are finite; a program needn't handle non-finite values.
Results may differ from a plain program's by a relative error of at most 0.0003.
Values may be sent and summed in bfloat16 or wider, within the bound.
No kernel may reach another device: no remote copies, remote signals or barrier semaphores. Data moves between devices by JAX's collectives and lax.ppermute only.
A program may use at most 64 MiB of HBM per device.

v0:
```python
import functools
import math

import jax
import jax.numpy as jnp
import numpy as np
from jax import lax
from jax.experimental import pallas as pl
from jax.experimental.pallas import tpu as pltpu
from jax.sharding import PartitionSpec as P

KEEP = 160
DT_STEP = 0.1
VISCOSITY = 0.05
LANES = 128
F32 = jnp.float32
BF16 = jnp.bfloat16

NN = (((1,), (0,)), ((), ()))
NT = (((1,), (1,)), ((), ()))


def round_up(value, unit):
    return -(-value // unit) * unit


def split_table(table):
    high = np.asarray(table, np.float32).astype(BF16)
    low = (np.asarray(table, np.float64) - high.astype(np.float64)).astype(np.float32).astype(BF16)
    return jnp.asarray(high), jnp.asarray(low)


def split_value(value):
    high = value.astype(BF16)
    return high, (value - high.astype(F32)).astype(BF16)


def dot3(left, right, dims):
    def one(a, b):
        return lax.dot_general(a, b, dims, preferred_element_type=F32)

    return one(left[0], right[0]) + (one(left[0], right[1]) + one(left[1], right[0]))


class Plan:
    def __init__(self, n, rows, space, count):
        self.n, self.rows, self.space, self.count = n, rows, space, count
        self.group = space // count
        self.block = round_up(-(-KEEP // self.group), 8)
        self.modes = self.block * self.group
        self.half = n // 2
        self.kpad = round_up(KEEP + 1, LANES)
        cells = np.arange(n) + 0.5
        scale = 2.0 * math.pi / n
        ky = np.arange(self.modes)
        live = (ky < KEEP)[:, None]
        angle_y = scale * ky[:, None] * cells[None, :]
        cos_y, sin_y = np.cos(angle_y) * live, np.sin(angle_y) * live
        self.y_forward = split_table(np.concatenate([cos_y, -sin_y], 0))
        twice = np.where(ky == 0, 1.0, 2.0)[:, None]
        inverse_y = np.stack([(cos_y * twice)[:, : self.half].T, (sin_y * twice)[:, : self.half].T])
        self.y_inverse = split_table(inverse_y)
        own = np.stack([2.0 * cos_y[:, : self.half], 2.0 * sin_y[:, : self.half]])
        own = own.reshape(2, self.group, self.block, self.half).transpose(1, 0, 2, 3)
        self.y_own = split_table(own)
        kx = np.arange(self.kpad)
        angle_x = scale * cells[:, None] * kx[None, :]
        keep_x = (kx <= KEEP)[None, :]
        self.x_table = split_table(np.concatenate([np.cos(angle_x) * keep_x, np.sin(angle_x) * keep_x], 1))


def rows_kernel(plan, field_ref, high_ref, low_ref, out_ref):
    rows, modes = plan.rows, plan.modes
    field = split_value(field_ref[...])
    partial = dot3((high_ref[...], low_ref[...]), field, NT)
    real, imag = partial[:modes], partial[modes:]
    for member in range(plan.count):
        at = slice(member * rows, (member + 1) * rows)
        packed = jnp.concatenate([real[:, at], imag[:, at]], 1)
        for peer in range(plan.group):
            out_ref[member * plan.group + peer] = packed


def project(plan, k_lane, cos_re, cos_im, sin_re, sin_im):
    weight = jnp.where((k_lane == 0) | (k_lane == KEEP), 1.0, 2.0)
    edge = jnp.where(k_lane == KEEP, 1.0, 0.0)
    return (
        weight * cos_re - edge * sin_im,
        weight * cos_im + edge * sin_re,
        weight * sin_re + edge * cos_im,
        weight * sin_im - edge * cos_re,
    )


def member_kernel(plan, own_ref, moved_ref, xh_ref, xl_ref, yih_ref, yil_ref, yoh_ref, yol_ref, out_ref, coef_ref):
    n, half, modes, block, kpad, rows = plan.n, plan.half, plan.modes, plan.block, plan.kpad, plan.rows
    unit = 2.0 * math.pi / n
    own = own_ref[0]

    def x_cos(at=slice(None)):
        return xh_ref[at, :kpad], xl_ref[at, :kpad]

    def x_sin(at=slice(None)):
        return xh_ref[at, kpad:], xl_ref[at, kpad:]

    real = jnp.concatenate([moved_ref[s, :, :rows] for s in range(plan.space)], 1)
    imag = jnp.concatenate([moved_ref[s, :, rows:] for s in range(plan.space)], 1)
    field = split_value(jnp.concatenate([real, imag], 0))
    spectrum = dot3(field, (xh_ref[...], xl_ref[...]), NN)
    sums = (spectrum[:modes, :kpad], spectrum[modes:, :kpad], spectrum[:modes, kpad:], spectrum[modes:, kpad:])
    for part in range(4):
        coef_ref[part] = sums[part]

    def waves(count, first):
        k_lane = lax.broadcasted_iota(jnp.int32, (count, kpad), 1)
        ky_row = lax.broadcasted_iota(jnp.int32, (count, kpad), 0) + first
        wave_x = k_lane.astype(F32) * unit
        wave_y = ky_row.astype(F32) * unit
        return k_lane, wave_x, wave_y, wave_x * wave_x + wave_y * wave_y

    k_lane, wave_x, wave_y, squared = waves(modes, 0)
    live = squared > 0
    inverse_sq = jnp.where(live, 1.0 / jnp.where(live, squared, 1.0), 0.0)
    a_re, a_im, b_re, b_im = project(plan, k_lane, *[s * (1.0 / (n * n)) for s in sums])
    pa_re, pa_im, pb_re, pb_im = (c * inverse_sq for c in (a_re, a_im, b_re, b_im))

    def to_cells(cos_part, sin_part):
        even = dot3(split_value(cos_part), x_cos(slice(0, half)), NT)
        odd = dot3(split_value(sin_part), x_sin(slice(0, half)), NT)
        both = jnp.concatenate([even + odd, even - odd], 1)
        cos_y = dot3((yih_ref[0], yil_ref[0]), split_value(both[:modes]), NN)
        sin_y = dot3((yih_ref[1], yil_ref[1]), split_value(both[modes:]), NN)
        return cos_y, sin_y

    rows_of = lambda re, im: jnp.concatenate([re, im], 0)
    w_cos, w_sin = to_cells(
        rows_of(jnp.where(live, a_re, 0.0), jnp.where(live, a_im, 0.0)), rows_of(b_re, b_im)
    )
    u_cos, u_sin = to_cells(
        rows_of(-wave_y * pa_im, wave_y * pa_re), rows_of(-wave_y * pb_im, wave_y * pb_re)
    )
    flux_u = ((u_cos * w_cos + u_sin * w_sin), (u_cos * w_sin + u_sin * w_cos))
    v_cos, v_sin = to_cells(
        rows_of(-wave_x * pb_re, -wave_x * pb_im), rows_of(wave_x * pa_re, wave_x * pa_im)
    )
    flux_v = ((v_cos * w_cos + v_sin * w_sin), (v_cos * w_sin + v_sin * w_cos))

    pieces = []
    for flux in (flux_u, flux_v):
        for part in range(2):
            pieces.append(dot3((yoh_ref[own, part], yol_ref[own, part]), split_value(flux[part]), NN))
    hats = jnp.concatenate(pieces, 0)
    hat_cos = dot3(split_value(hats[:, :half] + hats[:, half:]), x_cos(slice(0, half)), NN)
    hat_sin = dot3(split_value(hats[:, :half] - hats[:, half:]), x_sin(slice(0, half)), NN)
    cos1_re, cos1_im, cos2_re, cos2_im = (hat_cos[i * block : (i + 1) * block] for i in range(4))
    sin1_re, sin1_im, sin2_re, sin2_im = (hat_sin[i * block : (i + 1) * block] for i in range(4))

    first = pl.multiple_of(own * block, 8)
    k_lane, wave_x, wave_y, squared = waves(block, first)
    fade = 1.0 - (DT_STEP * VISCOSITY) * squared
    at = pl.ds(first, block)
    new = project(
        plan,
        k_lane,
        coef_ref[0, at, :] * fade - DT_STEP * (wave_x * sin1_re - wave_y * cos2_im),
        coef_ref[1, at, :] * fade - DT_STEP * (wave_x * sin1_im + wave_y * cos2_re),
        coef_ref[2, at, :] * fade - DT_STEP * (-wave_x * cos1_re - wave_y * sin2_im),
        coef_ref[3, at, :] * fade - DT_STEP * (-wave_x * cos1_im + wave_y * sin2_re),
    )
    line = dot3(split_value(rows_of(new[0], new[1])), x_cos(), NT) + dot3(
        split_value(rows_of(new[2], new[3])), x_sin(), NT
    )
    for peer in range(plan.space):
        cut = slice(peer * rows, (peer + 1) * rows)
        out_ref[peer] = jnp.concatenate([line[:block, cut], line[block:, cut]], 1)


def finish_kernel(plan, moved_ref, driving_ref, high_ref, low_ref, out_ref):
    rows, modes, n = plan.rows, plan.modes, plan.n
    ky = lax.broadcasted_iota(jnp.int32, (modes, 2 * rows), 0)
    weight = jnp.where(ky == 0, 1.0 / (n * n), 2.0 / (n * n))
    forcing = DT_STEP * driving_ref[...]
    cos_y = (high_ref[:modes], low_ref[:modes])
    sin_y = (high_ref[modes:], low_ref[modes:])
    for member in range(plan.count):
        line = moved_ref[member * plan.group : (member + 1) * plan.group].reshape(modes, 2 * rows)
        line = jnp.transpose(line * weight)
        fresh = dot3(split_value(line[:rows]), cos_y, NN) + dot3(split_value(line[rows:]), sin_y, NN)
        out_ref[member] = (fresh + forcing).astype(BF16)


def probe_kernel(rows, columns, probes_ref, observed_ref, count_ref, total_ref):
    probes = probes_ref[...]
    observed = observed_ref[...]
    amount = probes.shape[1]
    row, column = lax.div(probes, columns), lax.rem(probes, columns)
    in_row = lax.broadcasted_iota(jnp.int32, (rows, amount), 0) == row
    in_column = (lax.broadcasted_iota(jnp.int32, (columns, amount), 0) == column).astype(F32).astype(BF16)
    first = observed.astype(BF16)
    rest = observed - first.astype(F32)
    second = rest.astype(BF16)
    third = (rest - second.astype(F32)).astype(BF16)
    left = [in_row.astype(F32)]
    left += [jnp.where(in_row, piece.astype(F32), 0.0) for piece in (first, second, third)]
    left = jnp.concatenate(left, 0).astype(BF16)
    out = lax.dot_general(left, in_column, NT, preferred_element_type=F32)
    count_ref[...] = out[:rows]
    total_ref[...] = out[rows : 2 * rows] + (out[2 * rows : 3 * rows] + out[3 * rows :])


def analysis_kernel(count, copies, offset_ref, mixing_ref, values_ref, number_ref, total_ref, out_ref, part_ref, row_ref):
    members, rows, columns = values_ref.shape
    offset = offset_ref[0]
    values = [values_ref[j].astype(F32) for j in range(members)]
    state_sum = values[0]
    for j in range(1, members):
        state_sum = state_sum + values[j]
    for m in range(count):
        weights = [mixing_ref[j, offset + m] for j in range(members)]
        weight_sum = weights[0]
        for j in range(1, members):
            weight_sum = weight_sum + weights[j]
        acc = ((1.0 - weight_sum) * (1.0 / members)) * state_sum
        for j in range(members):
            acc = acc + weights[j] * values[j]
        out_ref[m] = acc
    number = number_ref[...]
    centre = state_sum * (1.0 / members)
    surprise = total_ref[...] - number * centre

    def to_row(product):
        line = jnp.sum(product, 0, keepdims=True)
        short = line[:, :LANES]
        for at in range(LANES, columns, LANES):
            short = short + line[:, at : at + LANES]
        return short

    anomaly = [v - centre for v in values]
    for i in range(members):
        weighted = anomaly[i] * number
        for j in range(i + 1):
            row = to_row(weighted * anomaly[j])
            row_ref[j, pl.ds(i, 1), :] = row
            if j != i:
                row_ref[i, pl.ds(j, 1), :] = row
        row_ref[members, pl.ds(i, 1), :] = to_row(anomaly[i] * surprise)
    lane = lax.broadcasted_iota(jnp.int32, (members, LANES), 1)
    tile = jnp.zeros((members, LANES), F32)
    for j in range(members + 1):
        tile = jnp.where(lane == j, jnp.sum(row_ref[j], 1, keepdims=True), tile)
    for peer in range(copies):
        part_ref[peer] = tile


def total_kernel(probes, parts_ref, spread_ref, projection_ref):
    copies, members, _ = parts_ref.shape
    total = parts_ref[0]
    for s in range(1, copies):
        total = total + parts_ref[s]
    spread_ref[...] = total[:, :members] * (1.0 / probes)
    projection_ref[...] = total[:, members : members + 1] * (1.0 / math.sqrt(probes))


def vmem(count):
    return [pl.BlockSpec(memory_space=pltpu.VMEM)] * count


SMEM = pl.BlockSpec(memory_space=pltpu.SMEM)


def on_device(plan, participant_swirls, driving_source, mixing, probes, observed):
    count, rows, n = participant_swirls.shape
    members, space = mixing.shape[0], plan.space
    own = (lax.axis_index("space") % plan.group).astype(jnp.int32).reshape(1)
    offset = (lax.axis_index("member") * count).astype(jnp.int32).reshape(1)
    y_high, y_low = plan.y_forward

    sent = pl.pallas_call(
        functools.partial(rows_kernel, plan),
        out_shape=jax.ShapeDtypeStruct((space, plan.modes, 2 * rows), F32),
        in_specs=vmem(3),
        out_specs=vmem(1)[0],
        name="rows_to_modes",
    )(participant_swirls.reshape(count * rows, n), y_high, y_low)
    moved = lax.all_to_all(sent, "space", split_axis=0, concat_axis=0, tiled=True)

    number, total = pl.pallas_call(
        functools.partial(probe_kernel, rows, n),
        out_shape=[jax.ShapeDtypeStruct((rows, n), F32)] * 2,
        in_specs=vmem(2),
        out_specs=vmem(2),
        name="probe_cells",
    )(probes.reshape(1, -1), observed.reshape(1, -1))

    line = pl.pallas_call(
        functools.partial(member_kernel, plan),
        out_shape=jax.ShapeDtypeStruct((space, plan.block, 2 * rows), F32),
        in_specs=[SMEM] + vmem(7),
        out_specs=vmem(1)[0],
        scratch_shapes=[pltpu.VMEM((4, plan.modes, plan.kpad), F32)],
        name="member_step",
    )(own, moved, *plan.x_table, *plan.y_inverse, *plan.y_own)
    moved = lax.all_to_all(line, "space", split_axis=0, concat_axis=0, tiled=True)

    rounded = pl.pallas_call(
        functools.partial(finish_kernel, plan),
        out_shape=jax.ShapeDtypeStruct((count, rows, n), BF16),
        in_specs=vmem(4),
        out_specs=vmem(1)[0],
        name="modes_to_rows",
    )(moved, driving_source, y_high, y_low)
    values = lax.all_gather(rounded, "member", axis=0, tiled=True)

    analysis, part = pl.pallas_call(
        functools.partial(analysis_kernel, count, space),
        out_shape=[
            jax.ShapeDtypeStruct((count, rows, n), F32),
            jax.ShapeDtypeStruct((space, members, LANES), F32),
        ],
        in_specs=[SMEM, SMEM] + vmem(3),
        out_specs=vmem(2),
        scratch_shapes=[pltpu.VMEM((members + 1, members, LANES), F32)],
        name="analysis",
    )(offset, mixing, values, number, total)
    parts = lax.all_to_all(part, "space", split_axis=0, concat_axis=0, tiled=True)
    spread, projection = pl.pallas_call(
        functools.partial(total_kernel, probes.shape[0] * space),
        out_shape=[jax.ShapeDtypeStruct((members, members), F32), jax.ShapeDtypeStruct((members, 1), F32)],
        in_specs=vmem(1),
        out_specs=vmem(2),
        name="probe_totals",
    )(parts)
    return analysis, spread, projection.reshape(members)


def solution(mesh):
    space = mesh.shape["space"]

    def body(participant_swirls, *rest):
        count, rows, n = participant_swirls.shape
        return on_device(Plan(n, rows, space, count), participant_swirls, *rest)

    return jax.shard_map(
        body,
        mesh=mesh,
        in_specs=(P("member", "space", None), P("space", None), P(), P("space"), P("space")),
        out_specs=(P("member", "space", None), P(), P()),
        check_vma=False,
    )
```

profile of v0, /device:TPU:0, one launch (start us, length us, event | category | flops | bytes accessed | tf_op | source)
XLA Modules:
  0.0 74.4 jit_solution(5183686993195162699)
XLA Ops:
  0.6 2.5 %rows_to_modes.1 = f32[8,160,128]{2,1,0:T(8,128)} custom-call(f32[128,512]{1,0:T(8,128)} %bitcast.5, bf16[320,512]{1,0:T(8,128)(2,1)} %constant.39.clone.high_ref, bf16[320,512]{1,0:T(8,128)(2,1)} %constant.40.clone.low_ref), custom_call_target="tpu_custom_call" | custom-call | tf_op jit(solution)/shard_map/rows_to_modes/pallas_call | solution.py:278
  3.1 7.3 %all-to-all-start = ((f32[8,160,128]{2,1,0:T(8,128)}), f32[8,160,128]{2,1,0:T(8,128)S(1)}, u32[]{:S(2)}, u32[]{:S(2)}) async-start(f32[8,160,128]{2,1,0:T(8,128)} %rows_to_modes.1), calls=%async_computation | async-start | bytes 1310720 | tf_op jit(solution)/shard_map/all_to_all | solution.py:285
  10.4 17.3 %all-to-all-done.moved_ref = f32[8,160,128]{2,1,0:T(8,128)S(1)} async-done(((f32[8,160,128]{2,1,0:T(8,128)}), f32[8,160,128]{2,1,0:T(8,128)S(1)}, u32[]{:S(2)}, u32[]{:S(2)}) %all-to-all-start) | async-done | bytes 655392 | tf_op jit(solution)/shard_map/all_to_all | solution.py:285
  27.7 0.0 copy-start
  27.7 0.8 %copy-done = f32[8,160,128]{2,1,0:T(8,128)} copy-done((f32[8,160,128]{2,1,0:T(8,128)}, f32[8,160,128]{2,1,0:T(8,128)S(1)}, u32[]{:S(2)}) %copy-start) | copy-done | bytes 655384
  28.5 7.2 %member_step.1 = f32[8,40,128]{2,1,0:T(8,128)} custom-call(s32[1]{0:T(128)} %bitcast.1.own_ref, f32[8,160,128]{2,1,0:T(8,128)} %copy-done, bf16[512,512]{1,0:T(8,128)(2,1)} %constant.45.clone.xh_ref, bf16[512,512]{1,0:T(8,128)(2,1)} %constant.46.clone.xl_ref, bf16[2,256,160]{2,1,0:T(8,128)(2,1)} %constant.41.clone.yih_ref, ...), custom_call_target="tpu_custom_call" | custom-call | tf_op jit(solution)/shard_map/member_step/pallas_call | solution.py:295
  35.7 3.6 %all-to-all-start.1 = ((f32[8,40,128]{2,1,0:T(8,128)}), f32[8,40,128]{2,1,0:T(8,128)S(1)}, u32[]{:S(2)}, u32[]{:S(2)}) async-start(f32[8,40,128]{2,1,0:T(8,128)} %member_step.1), calls=%async_computation.1 | async-start | bytes 327680 | tf_op jit(solution)/shard_map/all_to_all | solution.py:303
  39.3 2.1 %probe_cells.1 = (f32[64,512]{1,0:T(8,128)}, f32[64,512]{1,0:T(8,128)}) custom-call(s32[1,2048]{1,0:T(1,128)} %bitcast.6, f32[1,2048]{1,0:T(1,128)} %bitcast.7), custom_call_target="tpu_custom_call" | custom-call | tf_op jit(solution)/shard_map/probe_cells/pallas_call | solution.py:287
  41.5 5.5 %all-to-all-done.1.moved_ref = f32[8,40,128]{2,1,0:T(8,128)S(1)} async-done(((f32[8,40,128]{2,1,0:T(8,128)}), f32[8,40,128]{2,1,0:T(8,128)S(1)}, u32[]{:S(2)}, u32[]{:S(2)}) %all-to-all-start.1) | async-done | bytes 163872 | tf_op jit(solution)/shard_map/all_to_all | solution.py:303
  47.0 0.0 copy-start.1
  47.0 0.7 copy-done.1
  47.7 2.4 %modes_to_rows.1 = bf16[2,64,512]{2,1,0:T(8,128)(2,1)} custom-call(f32[8,40,128]{2,1,0:T(8,128)} %copy-done.1, f32[64,512]{1,0:T(8,128)} %driving_ref.1, bf16[320,512]{1,0:T(8,128)(2,1)} %constant.39.clone.high_ref, bf16[320,512]{1,0:T(8,128)(2,1)} %constant.40.clone.low_ref), custom_call_target="tpu_custom_call" | custom-call | tf_op jit(solution)/shard_map/modes_to_rows/pallas_call | solution.py:305
  50.1 8.1 %all_gather.3.values_ref = bf16[8,64,512]{2,1,0:T(8,128)(2,1)} all-gather(bf16[2,64,512]{2,1,0:T(8,128)(2,1)} %modes_to_rows.1), channel_id=1, replica_groups=mesh['member'=4,'space'=8] {'member'}, dimensions={0}, use_global_device_ids=true | all-gather | bytes 655360 | tf_op jit(solution)/shard_map/all_gather | solution.py:312
  58.2 2.8 %analysis.1 = (f32[2,64,512]{2,1,0:T(8,128)}, f32[8,8,128]{2,1,0:T(8,128)}) custom-call(s32[1]{0:T(128)} %bitcast.offset_ref, f32[8,8]{1,0:T(8,128)} %mixing_ref.1, bf16[8,64,512]{2,1,0:T(8,128)(2,1)} %all_gather.3.values_ref, f32[64,512]{1,0:T(8,128)} %get-tuple-element.9.number_ref, f32[64,512]{1,0:T(8,128)} %get-tuple-element.10.total_ref), custom_call_target="tpu_custom_call" | custom-call | tf_op jit(solution)/shard_map/analysis/pallas_call | solution.py:314
  61.0 10.6 %all_to_all.15.parts_ref = f32[8,8,128]{2,1,0:T(8,128)} all-to-all(f32[8,8,128]{2,1,0:T(8,128)} %get-tuple-element.12), channel_id=1, replica_groups=mesh['member'=4,'space'=8] {'space'}, dimensions={0} | all-to-all | bytes 65536 | tf_op jit(solution)/shard_map/all_to_all | solution.py:325
  71.6 1.4 %probe_totals.1 = (f32[8,8]{1,0:T(8,128)}, f32[8,1]{1,0:T(8,128)}) custom-call(f32[8,8,128]{2,1,0:T(8,128)} %all_to_all.15.parts_ref), custom_call_target="tpu_custom_call" | custom-call | tf_op jit(solution)/shard_map/probe_totals/pallas_call | solution.py:326
  73.1 1.3 %reduce = f32[8]{0:T(128)} reduce(f32[8,1]{1,0:T(8,128)} %get-tuple-element.14, f32[]{:T(128)} %constant.48), dimensions={1}, to_apply=%get-tuple-element.14.reduce_sub_computation | reduce | bytes 68 | tf_op jit(solution)/shard_map/probe_totals/pallas_call | solution.py:326
Async XLA Ops:
  3.1 24.6 %all-to-all-start = ((f32[8,160,128]{2,1,0:T(8,128)}), f32[8,160,128]{2,1,0:T(8,128)S(1)}, u32[]{:S(2)}, u32[]{:S(2)}) async-start(f32[8,160,128]{2,1,0:T(8,128)} %rows_to_modes.1), calls=%async_computation | async-start | bytes 1310720 | tf_op jit(solution)/shard_map/all_to_all | solution.py:285
  27.7 0.8 %copy-start = (f32[8,160,128]{2,1,0:T(8,128)}, f32[8,160,128]{2,1,0:T(8,128)S(1)}, u32[]{:S(2)}) copy-start(f32[8,160,128]{2,1,0:T(8,128)S(1)} %all-to-all-done.moved_ref) | copy-start | bytes 1966084
  35.7 11.3 %all-to-all-start.1 = ((f32[8,40,128]{2,1,0:T(8,128)}), f32[8,40,128]{2,1,0:T(8,128)S(1)}, u32[]{:S(2)}, u32[]{:S(2)}) async-start(f32[8,40,128]{2,1,0:T(8,128)} %member_step.1), calls=%async_computation.1 | async-start | bytes 327680 | tf_op jit(solution)/shard_map/all_to_all | solution.py:303
  47.0 0.7 copy-start.1
where the time goes:
time: 75 us; the launch traced here: 74.4 us
  waiting for transfers between devices  22.8 us (30%)
  blocking collectives  18.7 us (25%)
  Pallas kernels  18.4 us (25%)
  starting transfers between devices  10.9 us (15%)
  local copies, waits for them, and re-layouts  1.5 us (2%)
  other arithmetic  1.31 us (2%)
    all_to_all x1, waiting for transfers between devices, on_device(): lax.all_to_all(sent, 'space', split_axis=0, concat_axis=0, tiled=True)  17.3 us
    all_to_all x1, blocking collectives, on_device(): lax.all_to_all(part, 'space', split_axis=0, concat_axis=0, tiled=True)  10.6 us
    all_gather x1, blocking collectives, on_device(): values = lax.all_gather(rounded, 'member', axis=0, tiled=True)  8.12 us
    all_to_all x1, starting transfers between devices, on_device(): lax.all_to_all(sent, 'space', split_axis=0, concat_axis=0, tiled=True)  7.28 us
    pallas_call x1, Pallas kernels, on_device(): pl.pallas_call(functools.partial(member_kernel, plan), out_shape=jax.Shap...  7.17 us
    all_to_all x1, waiting for transfers between devices, on_device(): lax.all_to_all(line, 'space', split_axis=0, concat_axis=0, tiled=True)  5.55 us
    all_to_all x1, starting transfers between devices, on_device(): lax.all_to_all(line, 'space', split_axis=0, concat_axis=0, tiled=True)  3.64 us
    pallas_call x1, Pallas kernels, on_device(): pl.pallas_call(functools.partial(analysis_kernel, count, space), out_shap...  2.82 us
  transfers between devices with their start and end apart: 2, of which 2 were waited for; matrix products, arithmetic and copies ran while one was open for 0% of the time, Pallas kernels for 3%

commit v1 on v0

v1 whole, which is shorter than its diff:
```python
import functools
import math

import jax
import jax.numpy as jnp
import numpy as np
from jax import lax
from jax.experimental import pallas as pl
from jax.experimental.pallas import tpu as pltpu
from jax.sharding import PartitionSpec as P

KEEP = 160
DT_STEP = 0.1
VISCOSITY = 0.05
LANES = 128
F32 = jnp.float32
BF16 = jnp.bfloat16

NN = (((1,), (0,)), ((), ()))
NT = (((1,), (1,)), ((), ()))
FULL = ((0, 0), (0, 1), (1, 0), (1, 1), (0, 2), (2, 0))
SHORT = ((0, 0), (0, 1), (1, 0))
MIB = 1 << 20


def round_up(value, unit):
    return -(-value // unit) * unit


def split_table(table, pieces):
    rest, out = np.asarray(table, np.float64), []
    for _ in range(pieces):
        out.append(rest.astype(np.float32).astype(BF16))
        rest = rest - out[-1].astype(np.float64)
    return tuple(jnp.asarray(piece) for piece in out)


def split(value, pieces):
    out = []
    for piece in range(pieces):
        out.append(value.astype(BF16))
        if piece + 1 < pieces:
            value = value - out[-1].astype(F32)
    return out


def product(left, right, dims, terms):
    out = None
    for i, j in reversed(terms):
        term = lax.dot_general(left[i], right[j], dims, preferred_element_type=F32)
        out = term if out is None else out + term
    return out


class Plan:
    def __init__(self, n, rows, space, count):
        self.n, self.rows, self.space, self.count = n, rows, space, count
        self.group = space // count
        self.block = round_up(-(-KEEP // self.group), 8)
        self.modes = self.block * self.group
        self.half = n // 2
        self.kpad = round_up(KEEP + 1, LANES)
        cells = np.arange(n) + 0.5
        scale = 2.0 * math.pi / n
        ky = np.arange(self.modes)
        live = (ky < KEEP)[:, None]
        angle_y = scale * ky[:, None] * cells[None, :]
        cos_y, sin_y = np.cos(angle_y) * live, np.sin(angle_y) * live
        self.y_table = split_table(np.concatenate([cos_y, -sin_y], 0), 3)
        own = 2.0 * np.stack([cos_y, -sin_y])[:, :, : self.half]
        own = own.reshape(2, self.group, self.block, self.half).transpose(1, 0, 2, 3)
        self.y_own = split_table(own, 2)
        kx = np.arange(self.kpad)
        angle_x = scale * cells[:, None] * kx[None, :]
        keep_x = (kx <= KEEP)[None, :]
        self.x_table = split_table(np.concatenate([np.cos(angle_x) * keep_x, np.sin(angle_x) * keep_x], 1), 3)


def rows_kernel(plan, field_ref, y0_ref, y1_ref, y2_ref, out_ref):
    rows, modes = plan.rows, plan.modes
    field = split(field_ref[...], 3)
    partial = product((y0_ref[...], y1_ref[...], y2_ref[...]), field, NT, FULL)
    real, imag = partial[:modes], partial[modes:]
    for member in range(plan.count):
        at = slice(member * rows, (member + 1) * rows)
        packed = jnp.concatenate([real[:, at], imag[:, at]], 1)
        for peer in range(plan.group):
            out_ref[member * plan.group + peer] = packed


def project(plan, k_lane, cos_re, cos_im, sin_re, sin_im):
    weight = jnp.where((k_lane == 0) | (k_lane == KEEP), 1.0, 2.0)
    edge = jnp.where(k_lane == KEEP, 1.0, 0.0)
    return (
        weight * cos_re - edge * sin_im,
        weight * cos_im + edge * sin_re,
        weight * sin_re + edge * cos_im,
        weight * sin_im - edge * cos_re,
    )


def member_kernel(plan, own_ref, moved_ref, x0_ref, x1_ref, x2_ref, y0_ref, y1_ref, o0_ref, o1_ref, out_ref):
    n, half, modes, block, kpad, rows = plan.n, plan.half, plan.modes, plan.block, plan.kpad, plan.rows
    unit = 2.0 * math.pi / n
    own = own_ref[0]
    first = pl.multiple_of(own * block, 8)
    x_refs = (x0_ref, x1_ref, x2_ref)

    def x_cos(count, pieces):
        return [ref[:count, :kpad] for ref in x_refs[:pieces]]

    def x_sin(count, pieces):
        return [ref[:count, kpad:] for ref in x_refs[:pieces]]

    def gathered(at):
        real = jnp.concatenate([moved_ref[s, at, :rows] for s in range(plan.space)], 1)
        imag = jnp.concatenate([moved_ref[s, at, rows:] for s in range(plan.space)], 1)
        return jnp.concatenate([real, imag], 0)

    def parts(sums, count):
        return (sums[:count, :kpad], sums[count:, :kpad], sums[:count, kpad:], sums[count:, kpad:])

    def waves(count, start):
        k_lane = lax.broadcasted_iota(jnp.int32, (count, kpad), 1)
        ky_row = lax.broadcasted_iota(jnp.int32, (count, kpad), 0) + start
        wave_x = k_lane.astype(F32) * unit
        wave_y = ky_row.astype(F32) * unit
        return k_lane, ky_row, wave_x, wave_y, wave_x * wave_x + wave_y * wave_y

    x_pair = [x0_ref[...], x1_ref[...]]
    sums = parts(product(split(gathered(slice(0, modes)), 2), x_pair, NN, SHORT), modes)
    k_lane, ky_row, wave_x, wave_y, squared = waves(modes, 0)
    live = squared > 0
    inverse_sq = jnp.where(live, 1.0 / jnp.where(live, squared, 1.0), 0.0)
    weight = jnp.where(ky_row == 0, 1.0 / (n * n), 2.0 / (n * n))
    a_re, a_im, b_re, b_im = project(plan, k_lane, *[s * weight for s in sums])
    pa_re, pa_im, pb_re, pb_im = (c * inverse_sq for c in (a_re, a_im, b_re, b_im))
    y_cos = [jnp.transpose(ref[:modes, :half].astype(F32)).astype(BF16) for ref in (y0_ref, y1_ref)]
    y_sin = [jnp.transpose(ref[modes:, :half].astype(F32)).astype(BF16) for ref in (y0_ref, y1_ref)]

    def to_cells(cos_part, sin_part):
        even = product(split(cos_part, 2), x_cos(half, 2), NT, SHORT)
        odd = product(split(sin_part, 2), x_sin(half, 2), NT, SHORT)
        both = jnp.concatenate([even + odd, even - odd], 1)
        cos_y = product(y_cos, split(both[:modes], 2), NN, SHORT)
        sin_y = product(y_sin, split(both[modes:], 2), NN, SHORT)
        return cos_y, sin_y

    rows_of = lambda re, im: jnp.concatenate([re, im], 0)
    w_cos, w_sin = to_cells(
        rows_of(jnp.where(live, a_re, 0.0), jnp.where(live, a_im, 0.0)), rows_of(b_re, b_im)
    )
    u_cos, u_sin = to_cells(
        rows_of(-wave_y * pa_im, wave_y * pa_re), rows_of(-wave_y * pb_im, wave_y * pb_re)
    )
    flux_u = (u_cos * w_cos + u_sin * w_sin, u_cos * w_sin + u_sin * w_cos)
    v_cos, v_sin = to_cells(
        rows_of(-wave_x * pb_re, -wave_x * pb_im), rows_of(wave_x * pa_re, wave_x * pa_im)
    )
    flux_v = (v_cos * w_cos + v_sin * w_sin, v_cos * w_sin + v_sin * w_cos)

    pieces = []
    for flux in (flux_u, flux_v):
        for part in range(2):
            pieces.append(product((o0_ref[own, part], o1_ref[own, part]), split(flux[part], 2), NN, SHORT))
    hats = jnp.concatenate(pieces, 0)
    hat_cos = product(split(hats[:, :half] + hats[:, half:], 2), x_cos(half, 2), NN, SHORT)
    hat_sin = product(split(hats[:, :half] - hats[:, half:], 2), x_sin(half, 2), NN, SHORT)
    cos1_re, cos1_im, cos2_re, cos2_im = (hat_cos[i * block : (i + 1) * block] for i in range(4))
    sin1_re, sin1_im, sin2_re, sin2_im = (hat_sin[i * block : (i + 1) * block] for i in range(4))

    mine = product(split(gathered(pl.ds(first, block)), 3), [ref[...] for ref in x_refs], NN, FULL)
    mine = parts(mine, block)
    k_lane, _, wave_x, wave_y, squared = waves(block, first)
    fade = 1.0 - (DT_STEP * VISCOSITY) * squared
    new = project(
        plan,
        k_lane,
        mine[0] * fade - DT_STEP * (wave_x * sin1_re - wave_y * cos2_im),
        mine[1] * fade - DT_STEP * (wave_x * sin1_im + wave_y * cos2_re),
        mine[2] * fade - DT_STEP * (-wave_x * cos1_re - wave_y * sin2_im),
        mine[3] * fade - DT_STEP * (-wave_x * cos1_im + wave_y * sin2_re),
    )
    line = product(split(rows_of(new[0], new[1]), 3), x_cos(n, 3), NT, FULL) + product(
        split(rows_of(new[2], new[3]), 3), x_sin(n, 3), NT, FULL
    )
    for peer in range(plan.space):
        cut = slice(peer * rows, (peer + 1) * rows)
        out_ref[peer] = jnp.concatenate([line[:block, cut], line[block:, cut]], 1)


def finish_kernel(plan, moved_ref, driving_ref, y0_ref, y1_ref, y2_ref, out_ref):
    rows, modes, n, count = plan.rows, plan.modes, plan.n, plan.count
    ky = lax.broadcasted_iota(jnp.int32, (modes, 2 * rows), 0)
    weight = jnp.where(ky == 0, 1.0 / (n * n), 2.0 / (n * n))
    lines = []
    for member in range(count):
        line = moved_ref[member * plan.group : (member + 1) * plan.group].reshape(modes, 2 * rows)
        lines.append(jnp.transpose(line * weight))
    real = jnp.concatenate([line[:rows] for line in lines], 0)
    imag = jnp.concatenate([line[rows:] for line in lines], 0)
    y_refs = (y0_ref, y1_ref, y2_ref)
    fresh = product(split(real, 3), [ref[:modes] for ref in y_refs], NN, FULL)
    fresh = fresh + product(split(imag, 3), [ref[modes:] for ref in y_refs], NN, FULL)
    forcing = DT_STEP * driving_ref[...]
    for member in range(count):
        out_ref[member] = (fresh[member * rows : (member + 1) * rows] + forcing).astype(BF16)


def probe_kernel(rows, columns, probes_ref, observed_ref, count_ref, total_ref):
    probes = probes_ref[...]
    observed = observed_ref[...]
    amount = probes.shape[1]
    row, column = lax.div(probes, columns), lax.rem(probes, columns)
    in_row = lax.broadcasted_iota(jnp.int32, (rows, amount), 0) == row
    in_column = (lax.broadcasted_iota(jnp.int32, (columns, amount), 0) == column).astype(F32).astype(BF16)
    first = observed.astype(BF16)
    rest = observed - first.astype(F32)
    second = rest.astype(BF16)
    third = (rest - second.astype(F32)).astype(BF16)
    left = [in_row.astype(F32)]
    left += [jnp.where(in_row, piece.astype(F32), 0.0) for piece in (first, second, third)]
    left = jnp.concatenate(left, 0).astype(BF16)
    out = lax.dot_general(left, in_column, NT, preferred_element_type=F32)
    count_ref[...] = out[:rows]
    total_ref[...] = out[rows : 2 * rows] + (out[2 * rows : 3 * rows] + out[3 * rows :])


def state_sum_of(values):
    total = values[0]
    for value in values[1:]:
        total = total + value
    return total


def analysis_kernel(count, offset_ref, mixing_ref, values_ref, out_ref):
    members = values_ref.shape[0]
    offset = offset_ref[0]
    values = [values_ref[j].astype(F32) for j in range(members)]
    state_sum = state_sum_of(values)
    for m in range(count):
        weights = [mixing_ref[j, offset + m] for j in range(members)]
        acc = ((1.0 - state_sum_of(weights)) * (1.0 / members)) * state_sum
        for j in range(members):
            acc = acc + weights[j] * values[j]
        out_ref[m] = acc


def products_kernel(copies, values_ref, number_ref, total_ref, part_ref, row_ref):
    members, rows, columns = values_ref.shape
    values = [values_ref[j].astype(F32) for j in range(members)]
    number = number_ref[...]
    centre = state_sum_of(values) * (1.0 / members)
    surprise = total_ref[...] - number * centre

    def to_row(product):
        line = jnp.sum(product, 0, keepdims=True)
        short = line[:, :LANES]
        for at in range(LANES, columns, LANES):
            short = short + line[:, at : at + LANES]
        return short

    anomaly = [v - centre for v in values]
    for i in range(members):
        weighted = anomaly[i] * number
        for j in range(i + 1):
            row = to_row(weighted * anomaly[j])
            row_ref[j, pl.ds(i, 1), :] = row
            if j != i:
                row_ref[i, pl.ds(j, 1), :] = row
        row_ref[members, pl.ds(i, 1), :] = to_row(anomaly[i] * surprise)
    lane = lax.broadcasted_iota(jnp.int32, (members, LANES), 1)
    tile = jnp.zeros((members, LANES), F32)
    for j in range(members + 1):
        tile = jnp.where(lane == j, jnp.sum(row_ref[j], 1, keepdims=True), tile)
    for peer in range(copies):
        part_ref[peer] = tile


def total_kernel(probes, parts_ref, spread_ref, projection_ref):
    copies, members, lanes = parts_ref.shape
    total = parts_ref[0]
    for s in range(1, copies):
        total = total + parts_ref[s]
    spread_ref[...] = total[:, :members] * (1.0 / probes)
    lane = lax.broadcasted_iota(jnp.int32, (members, lanes), 1)
    row = lax.broadcasted_iota(jnp.int32, (members, lanes), 0)
    column = jnp.where(lane == row, total[:, members : members + 1], 0.0)
    projection_ref[...] = jnp.sum(column, 0, keepdims=True)[:, :members] * (1.0 / math.sqrt(probes))


VMEM = pl.BlockSpec(memory_space=pltpu.VMEM)
SMEM = pl.BlockSpec(memory_space=pltpu.SMEM)


def local(kernel, name, limit, in_specs, out_shape, scratch=()):
    return pl.pallas_call(
        kernel,
        out_shape=out_shape,
        in_specs=in_specs,
        out_specs=jax.tree.map(lambda _: VMEM, out_shape),
        scratch_shapes=scratch,
        compiler_params=pltpu.CompilerParams(vmem_limit_bytes=limit * MIB),
        name=name,
    )


def on_device(plan, participant_swirls, driving_source, mixing, probes, observed):
    count, rows, n = participant_swirls.shape
    members, space = mixing.shape[0], plan.space
    array = jax.ShapeDtypeStruct
    own = (lax.axis_index("space") % plan.group).astype(jnp.int32).reshape(1)
    offset = (lax.axis_index("member") * count).astype(jnp.int32).reshape(1)
    exchange = functools.partial(lax.all_to_all, axis_name="space", split_axis=0, concat_axis=0, tiled=True)

    sent = local(
        functools.partial(rows_kernel, plan), "rows_to_modes", 8, [VMEM] * 4,
        array((space, plan.modes, 2 * rows), F32),
    )(participant_swirls.reshape(count * rows, n), *plan.y_table)
    moved = exchange(sent)
    number, total = local(
        functools.partial(probe_kernel, rows, n), "probe_cells", 16, [VMEM] * 2, [array((rows, n), F32)] * 2
    )(probes.reshape(1, -1), observed.reshape(1, -1))
    line = local(
        functools.partial(member_kernel, plan), "member_step", 24, [SMEM] + [VMEM] * 8,
        array((space, plan.block, 2 * rows), F32),
    )(own, moved, *plan.x_table, *plan.y_table[:2], *plan.y_own)
    moved = exchange(line)
    rounded = local(
        functools.partial(finish_kernel, plan), "modes_to_rows", 8, [VMEM] * 5, array((count, rows, n), BF16)
    )(moved, driving_source, *plan.y_table)
    values = lax.all_gather(rounded, "member", axis=0, tiled=True)
    part = local(
        functools.partial(products_kernel, space), "products", 16, [VMEM] * 3,
        array((space, members, LANES), F32),
        [pltpu.VMEM((members + 1, members, LANES), F32)],
    )(values, number, total)
    parts = exchange(part)
    analysis = local(
        functools.partial(analysis_kernel, count), "analysis", 16, [SMEM, SMEM, VMEM], array((count, rows, n), F32)
    )(offset, mixing, values)
    spread, projection = local(
        functools.partial(total_kernel, probes.shape[0] * space), "probe_totals", 4, [VMEM],
        [array((members, members), F32), array((1, members), F32)],
    )(parts)
    return analysis, spread, projection.reshape(members)


def solution(mesh):
    space = mesh.shape["space"]

    def body(participant_swirls, *rest):
        count, rows, n = participant_swirls.shape
        return on_device(Plan(n, rows, space, count), participant_swirls, *rest)

    return jax.shard_map(
        body,
        mesh=mesh,
        in_specs=(P("member", "space", None), P("space", None), P(), P("space"), P("space")),
        out_specs=(P("member", "space", None), P(), P()),
        check_vma=False,
    )
```

time: 75 us -> 69.2 us (0.923)
  blocking collectives: 18.7 us -> 7.2 us
  waiting for transfers between devices: 22.8 us -> 28.6 us
  Pallas kernels: 18.4 us -> 13 us
  starting transfers between devices: 10.9 us -> 14.5 us
  local copies, waits for them, and re-layouts: 1.5 us -> 4.59 us
  other arithmetic: 1.31 us -> 0 us
    all_to_all x1 -> x0, blocking collectives: 10.6 us -> none  [on_device(): lax.all_to_all(part, 'space', split_axis=0, concat_axis=0, tiled=True)]
    all_to_all x2 -> x3, waiting for transfers between devices: 22.8 us -> 28.6 us  [the longest x1 17.3 us: on_device(): moved = exchange(sent)]
    pallas_call x6 -> x7, Pallas kernels: 18.4 us -> 13 us  [the longest x1 6.41 us: on_device(): local(functools.partial(member_kernel, plan), 'member_step', 24, [SMEM] +...]
    all_to_all x2 -> x3, starting transfers between devices: 10.9 us -> 14.5 us  [the longest x1 7.41 us: on_device(): moved = exchange(sent)]
    unnamed x4 -> x32, local copies, waits for them, and re-layouts: 1.5 us -> 4.59 us
    pallas_call x1 -> x0, other arithmetic: 1.31 us -> none  [on_device(): pl.pallas_call(functools.partial(total_kernel, probes.shape[0] * space),...]
    all_gather x1, blocking collectives: 8.12 us -> 7.2 us  [on_device(): values = lax.all_gather(rounded, 'member', axis=0, tiled=True)]
  transfers between devices with their start and end apart: 2 -> 3, of which waited for: 2 -> 3; matrix products, arithmetic and copies ran while one was open for 0% -> 0% of each run, Pallas kernels for 3% -> 3%
where the time goes in v1:
time: 69.2 us; the launch traced here: 68.7 us
  waiting for transfers between devices  28.6 us (41%)
  starting transfers between devices  14.5 us (21%)
  Pallas kernels  13 us (19%)
  blocking collectives  7.2 us (10%)
  local copies, waits for them, and re-layouts  4.59 us (7%)
  between operations  0.76 us (1%)
    all_to_all x1, waiting for transfers between devices, on_device(): moved = exchange(sent)  17.3 us
    all_to_all x1, starting transfers between devices, on_device(): moved = exchange(sent)  7.41 us
    all_gather x1, blocking collectives, on_device(): values = lax.all_gather(rounded, 'member', axis=0, tiled=True)  7.2 us
    all_to_all x1, waiting for transfers between devices, on_device(): moved = exchange(line)  6.88 us
    pallas_call x1, Pallas kernels, on_device(): local(functools.partial(member_kernel, plan), 'member_step', 24, [SMEM] +...  6.41 us
    unnamed x32, local copies, waits for them, and re-layouts  4.59 us
    all_to_all x1, waiting for transfers between devices, on_device(): parts = exchange(part)  4.41 us
    all_to_all x1, starting transfers between devices, on_device(): moved = exchange(line)  3.77 us
  transfers between devices with their start and end apart: 3, of which 3 were waited for; matrix products, arithmetic and copies ran while one was open for 0% of the time, Pallas kernels for 3%

profile of v1, /device:TPU:0, one launch (start us, length us, event | category | flops | bytes accessed | tf_op | source)
XLA Modules:
  0.0 68.7 jit_solution(13491133066885484242)
XLA Ops:
  0.6 0.0 copy-start
  0.6 1.0 %copy-done = bf16[320,512]{1,0:T(8,128)(2,1)S(1)} copy-done((bf16[320,512]{1,0:T(8,128)(2,1)S(1)}, bf16[320,512]{1,0:T(8,128)(2,1)}, u32[]{:S(2)}) %copy-start) | copy-done | bytes 327704
  1.6 0.0 copy-start.2
  1.6 1.0 %copy-done.2 = bf16[320,512]{1,0:T(8,128)(2,1)S(1)} copy-done((bf16[320,512]{1,0:T(8,128)(2,1)S(1)}, bf16[320,512]{1,0:T(8,128)(2,1)}, u32[]{:S(2)}) %copy-start.2) | copy-done | bytes 327704
  2.6 0.0 copy-start.4
  2.6 1.0 %copy-done.4 = bf16[320,512]{1,0:T(8,128)(2,1)S(1)} copy-done((bf16[320,512]{1,0:T(8,128)(2,1)S(1)}, bf16[320,512]{1,0:T(8,128)(2,1)}, u32[]{:S(2)}) %copy-start.4) | copy-done | bytes 327704
  3.6 0.0 copy-start.9
  3.6 0.9 %copy-done.9 = f32[2,64,512]{2,1,0:T(8,128)S(1)} copy-done((f32[2,64,512]{2,1,0:T(8,128)S(1)}, f32[2,64,512]{2,1,0:T(8,128)}, u32[]{:S(2)}) %copy-start.9) | copy-done | bytes 262168
  4.5 0.0 copy-start.7
  4.5 0.0 copy-start.8
  4.5 0.0 copy-start.10
  4.5 0.0 copy-start.11
  4.5 1.6 %rows_to_modes.1 = f32[8,160,128]{2,1,0:T(8,128)} custom-call(f32[128,512]{1,0:T(8,128)S(1)} %bitcast.6, bf16[320,512]{1,0:T(8,128)(2,1)S(1)} %copy-done, bf16[320,512]{1,0:T(8,128)(2,1)S(1)} %copy-done.2, bf16[320,512]{1,0:T(8,128)(2,1)S(1)} %copy-done.4), custom_call_target="tpu_custom_call" | custom-call | tf_op jit(solution)/shard_map/rows_to_modes/pallas_call | solution.py:316
  6.1 0.0 copy-start.1
  6.1 0.0 copy-start.3
  6.1 0.0 copy-start.6
  6.1 7.4 %all-to-all-start = ((f32[8,160,128]{2,1,0:T(8,128)}), f32[8,160,128]{2,1,0:T(8,128)S(1)}, u32[]{:S(2)}, u32[]{:S(2)}) async-start(f32[8,160,128]{2,1,0:T(8,128)} %rows_to_modes.1), calls=%async_computation | async-start | bytes 1310720 | tf_op jit(solution)/shard_map/all_to_all | solution.py:320
  13.6 17.3 %all-to-all-done.moved_ref = f32[8,160,128]{2,1,0:T(8,128)S(1)} async-done(((f32[8,160,128]{2,1,0:T(8,128)}), f32[8,160,128]{2,1,0:T(8,128)S(1)}, u32[]{:S(2)}, u32[]{:S(2)}) %all-to-all-start) | async-done | bytes 655392 | tf_op jit(solution)/shard_map/all_to_all | solution.py:320
  30.9 0.0 copy-done.7
  30.9 0.0 copy-done.8
  30.9 0.0 copy-done.10
  30.9 0.0 copy-done.11
  30.9 0.0 copy-done.1
  30.9 0.0 copy-done.3
  30.9 0.0 copy-done.6
  30.9 0.0 copy-start.13
  30.9 0.0 copy-start.14
  30.9 0.0 copy-start.12
  30.9 6.4 %member_step.1 = f32[8,40,128]{2,1,0:T(8,128)} custom-call(s32[1]{0:T(128)} %bitcast.1.own_ref, f32[8,160,128]{2,1,0:T(8,128)S(1)} %all-to-all-done.moved_ref, bf16[512,512]{1,0:T(8,128)(2,1)S(1)} %copy-done.6, bf16[512,512]{1,0:T(8,128)(2,1)S(1)} %copy-done.7, bf16[512,512]{1,0:T(8,128)(2,1)S(1)} %copy-done.8, bf16[320,512]{1,0:T(8,128)(2,1)S(1)} %copy-done.1, ...), custom_call_target="tpu_custom_call" | custom-call | tf_op jit(solution)/shard_map/member_step/pallas_call | solution.py:324
  37.4 0.0 copy-start.5
  37.4 3.8 %all-to-all-start.1 = ((f32[8,40,128]{2,1,0:T(8,128)}), f32[8,40,128]{2,1,0:T(8,128)S(1)}, u32[]{:S(2)}, u32[]{:S(2)}) async-start(f32[8,40,128]{2,1,0:T(8,128)} %member_step.1), calls=%async_computation.1 | async-start | bytes 327680 | tf_op jit(solution)/shard_map/all_to_all | solution.py:328
  41.1 0.0 copy-done.13
  41.1 0.0 copy-done.14
  41.1 0.7 %probe_cells.1 = (f32[64,512]{1,0:T(8,128)S(1)}, f32[64,512]{1,0:T(8,128)S(1)}) custom-call(s32[1,2048]{1,0:T(1,128)S(1)} %bitcast.7, f32[1,2048]{1,0:T(1,128)S(1)} %bitcast.8), custom_call_target="tpu_custom_call" | custom-call | tf_op jit(solution)/shard_map/probe_cells/pallas_call | solution.py:321
  41.9 6.9 %all-to-all-done.1.moved_ref = f32[8,40,128]{2,1,0:T(8,128)S(1)} async-done(((f32[8,40,128]{2,1,0:T(8,128)}), f32[8,40,128]{2,1,0:T(8,128)S(1)}, u32[]{:S(2)}, u32[]{:S(2)}) %all-to-all-start.1) | async-done | bytes 163872 | tf_op jit(solution)/shard_map/all_to_all | solution.py:328
  48.8 0.0 copy-done.12
  48.8 0.0 copy-done.5
  48.8 0.6 modes_to_rows.1
  49.4 7.2 %all_gather.3.values_ref = bf16[8,64,512]{2,1,0:T(8,128)(2,1)S(1)} all-gather(bf16[2,64,512]{2,1,0:T(8,128)(2,1)S(1)} %modes_to_rows.1), channel_id=1, replica_groups=mesh['member'=4,'space'=8] {'member'}, dimensions={0}, use_global_device_ids=true | all-gather | bytes 655360 | tf_op jit(solution)/shard_map/all_gather | solution.py:332
  56.6 1.5 %products.1 = f32[8,8,128]{2,1,0:T(8,128)} custom-call(bf16[8,64,512]{2,1,0:T(8,128)(2,1)S(1)} %all_gather.3.values_ref, f32[64,512]{1,0:T(8,128)S(1)} %get-tuple-element.7.number_ref, f32[64,512]{1,0:T(8,128)S(1)} %get-tuple-element.8.total_ref), custom_call_target="tpu_custom_call" | custom-call | tf_op jit(solution)/shard_map/products/pallas_call | solution.py:333
  58.1 3.3 %all-to-all-start.2 = ((f32[8,8,128]{2,1,0:T(8,128)}), f32[8,8,128]{2,1,0:T(8,128)S(1)}, u32[]{:S(2)}, u32[]{:S(2)}) async-start(f32[8,8,128]{2,1,0:T(8,128)} %products.1), calls=%async_computation.2 | async-start | bytes 65536 | tf_op jit(solution)/shard_map/all_to_all | solution.py:338
  61.5 0.0 copy-start.15
  61.5 0.7 copy-done.15
  62.2 1.5 %analysis.1 = f32[2,64,512]{2,1,0:T(8,128)} custom-call(s32[1]{0:T(128)} %bitcast.offset_ref, f32[8,8]{1,0:T(8,128)S(1)} %copy-done.15, bf16[8,64,512]{2,1,0:T(8,128)(2,1)S(1)} %all_gather.3.values_ref), custom_call_target="tpu_custom_call" | custom-call | tf_op jit(solution)/shard_map/analysis/pallas_call | solution.py:339
  63.7 4.4 %all-to-all-done.2.parts_ref = f32[8,8,128]{2,1,0:T(8,128)S(1)} async-done(((f32[8,8,128]{2,1,0:T(8,128)}), f32[8,8,128]{2,1,0:T(8,128)S(1)}, u32[]{:S(2)}, u32[]{:S(2)}) %all-to-all-start.2) | async-done | bytes 32800 | tf_op jit(solution)/shard_map/all_to_all | solution.py:338
  68.1 0.6 probe_totals.1
Async XLA Ops:
  0.6 1.0 %copy-start = (bf16[320,512]{1,0:T(8,128)(2,1)S(1)}, bf16[320,512]{1,0:T(8,128)(2,1)}, u32[]{:S(2)}) copy-start(bf16[320,512]{1,0:T(8,128)(2,1)} %constant.39.clone.y0_ref) | copy-start | bytes 983044
  1.6 1.0 %copy-start.2 = (bf16[320,512]{1,0:T(8,128)(2,1)S(1)}, bf16[320,512]{1,0:T(8,128)(2,1)}, u32[]{:S(2)}) copy-start(bf16[320,512]{1,0:T(8,128)(2,1)} %constant.40.clone.y1_ref) | copy-start | bytes 983044
  2.6 1.0 %copy-start.4 = (bf16[320,512]{1,0:T(8,128)(2,1)S(1)}, bf16[320,512]{1,0:T(8,128)(2,1)}, u32[]{:S(2)}) copy-start(bf16[320,512]{1,0:T(8,128)(2,1)} %constant.41.clone.y2_ref) | copy-start | bytes 983044
  3.6 0.9 %copy-start.9 = (f32[2,64,512]{2,1,0:T(8,128)S(1)}, f32[2,64,512]{2,1,0:T(8,128)}, u32[]{:S(2)}) copy-start(f32[2,64,512]{2,1,0:T(8,128)} %param.13) | copy-start | bytes 786436
  4.5 26.4 %copy-start.7 = (bf16[512,512]{1,0:T(8,128)(2,1)S(1)}, bf16[512,512]{1,0:T(8,128)(2,1)}, u32[]{:S(2)}) copy-start(bf16[512,512]{1,0:T(8,128)(2,1)} %constant.45.clone.x1_ref) | copy-start | bytes 1572868
  4.5 26.4 %copy-start.8 = (bf16[512,512]{1,0:T(8,128)(2,1)S(1)}, bf16[512,512]{1,0:T(8,128)(2,1)}, u32[]{:S(2)}) copy-start(bf16[512,512]{1,0:T(8,128)(2,1)} %constant.46.clone.x2_ref) | copy-start | bytes 1572868
  4.5 26.4 %copy-start.10 = (bf16[4,2,40,256]{3,2,1,0:T(8,128)(2,1)S(1)}, bf16[4,2,40,256]{3,2,1,0:T(8,128)(2,1)}, u32[]{:S(2)}) copy-start(bf16[4,2,40,256]{3,2,1,0:T(8,128)(2,1)} %constant.42.clone.o0_ref) | copy-start | bytes 491524
  4.5 26.4 %copy-start.11 = (bf16[4,2,40,256]{3,2,1,0:T(8,128)(2,1)S(1)}, bf16[4,2,40,256]{3,2,1,0:T(8,128)(2,1)}, u32[]{:S(2)}) copy-start(bf16[4,2,40,256]{3,2,1,0:T(8,128)(2,1)} %constant.43.clone.o1_ref) | copy-start | bytes 491524
  6.1 24.7 %copy-start.1 = (bf16[320,512]{1,0:T(8,128)(2,1)S(1)}, bf16[320,512]{1,0:T(8,128)(2,1)}, u32[]{:S(2)}) copy-start(bf16[320,512]{1,0:T(8,128)(2,1)} %constant.39.clone.y0_ref) | copy-start | bytes 983044
  6.1 24.7 %copy-start.3 = (bf16[320,512]{1,0:T(8,128)(2,1)S(1)}, bf16[320,512]{1,0:T(8,128)(2,1)}, u32[]{:S(2)}) copy-start(bf16[320,512]{1,0:T(8,128)(2,1)} %constant.40.clone.y1_ref) | copy-start | bytes 983044
  6.1 24.8 %copy-start.6 = (bf16[512,512]{1,0:T(8,128)(2,1)S(1)}, bf16[512,512]{1,0:T(8,128)(2,1)}, u32[]{:S(2)}) copy-start(bf16[512,512]{1,0:T(8,128)(2,1)} %constant.44.clone.x0_ref) | copy-start | bytes 1572868
  6.1 24.7 %all-to-all-start = ((f32[8,160,128]{2,1,0:T(8,128)}), f32[8,160,128]{2,1,0:T(8,128)S(1)}, u32[]{:S(2)}, u32[]{:S(2)}) async-start(f32[8,160,128]{2,1,0:T(8,128)} %rows_to_modes.1), calls=%async_computation | async-start | bytes 1310720 | tf_op jit(solution)/shard_map/all_to_all | solution.py:320
  30.9 10.2 %copy-start.13 = (s32[2048]{0:T(1024)S(1)}, s32[2048]{0:T(1024)}, u32[]{:S(2)}) copy-start(s32[2048]{0:T(1024)} %param.16) | copy-start | bytes 24580
  30.9 10.2 %copy-start.14 = (f32[2048]{0:T(1024)S(1)}, f32[2048]{0:T(1024)}, u32[]{:S(2)}) copy-start(f32[2048]{0:T(1024)} %param.17) | copy-start | bytes 24580
  30.9 17.8 %copy-start.12 = (f32[64,512]{1,0:T(8,128)S(1)}, f32[64,512]{1,0:T(8,128)}, u32[]{:S(2)}) copy-start(f32[64,512]{1,0:T(8,128)} %driving_ref.1) | copy-start | bytes 393220
  37.4 11.4 %copy-start.5 = (bf16[320,512]{1,0:T(8,128)(2,1)S(1)}, bf16[320,512]{1,0:T(8,128)(2,1)}, u32[]{:S(2)}) copy-start(bf16[320,512]{1,0:T(8,128)(2,1)} %constant.41.clone.y2_ref) | copy-start | bytes 983044
  37.4 11.4 %all-to-all-start.1 = ((f32[8,40,128]{2,1,0:T(8,128)}), f32[8,40,128]{2,1,0:T(8,128)S(1)}, u32[]{:S(2)}, u32[]{:S(2)}) async-start(f32[8,40,128]{2,1,0:T(8,128)} %member_step.1), calls=%async_computation.1 | async-start | bytes 327680 | tf_op jit(solution)/shard_map/all_to_all | solution.py:328
  58.1 10.0 %all-to-all-start.2 = ((f32[8,8,128]{2,1,0:T(8,128)}), f32[8,8,128]{2,1,0:T(8,128)S(1)}, u32[]{:S(2)}, u32[]{:S(2)}) async-start(f32[8,8,128]{2,1,0:T(8,128)} %products.1), calls=%async_computation.2 | async-start | bytes 65536 | tf_op jit(solution)/shard_map/all_to_all | solution.py:338
  61.5 0.7 %copy-start.15 = (f32[8,8]{1,0:T(8,128)S(1)}, f32[8,8]{1,0:T(8,128)}, u32[]{:S(2)}) copy-start(f32[8,8]{1,0:T(8,128)} %mixing_ref.1) | copy-start | bytes 772
